TPU v7x, 128 devices: a whole 4x4x4 slice. The times are simulated.
128 devices in a mesh: blk: 16 (over z, x_hi, core), head: 8 (over y, x_lo).
Axes of the slice: x: 4 (x_hi: 2, x_lo: 2; x = x_hi * 2 + x_lo), y: 4, z: 4, core: 2. Of those that a mesh axis runs over, the one named last changes fastest.
Arguments:
- queries: bfloat16 [4096, 8192], P('blk', 'head'), may hold values from -4 to 10
- context_keys: bfloat16 [16384, 1024], P('blk', 'head'), may hold values from -4 to 7
- context_values: bfloat16 [16384, 1024], P('blk', 'head'), may hold values from -6 to 6
- response_keys: bfloat16 [4096, 1024], P('blk', 'head'), may hold values from -4 to 7
- response_values: bfloat16 [4096, 1024], P('blk', 'head'), may hold values from -6 to 6
- out_weight: bfloat16 [8192, 8192], P('head', 'blk'), may hold values from -0.09375 to 0.09375
- query_docs: int32 [32], replicated, may hold values from 0 to 2
- block_docs: int32 [128], replicated, may hold values from 0 to 2
- visits: int32 [32, 4, 8], replicated, may hold values 0 or 1
Outputs:
- mixed: bfloat16 [4096, 8192], P('blk', 'head')
All inputs are finite; a program needn't handle non-finite values.
Results may differ from a plain program's by a relative error of at most 0.0165.
Values may be sent and summed in bfloat16 or wider, within the bound.
No kernel may reach another device: no remote copies, remote signals or barrier semaphores. Data moves between devices by JAX's collectives and lax.ppermute only.
A program may use at most 128 MiB of HBM per device.

v0:
```python
import jax
import jax.numpy as jnp
from jax import lax
from jax.sharding import PartitionSpec as P

HQ = 64
KVH = 8
HD = 128
BLOCK = 128
HOPS = 3


def from_behind(value, axis, by):
    devices = lax.axis_size(axis)
    return lax.ppermute(value, axis, [(i, (i + by) % devices) for i in range(devices)])


def attend(running, highest, weight_sum, query_heads, key_block, value_block, allowed):
    rows_here, heads_here, per_group, width = query_heads.shape
    key_heads = key_block.reshape(-1, heads_here, width)
    value_heads = value_block.reshape(-1, heads_here, width)
    scores = jnp.einsum(
        "tgjd,sgd->tgjs", query_heads, key_heads, preferred_element_type=jnp.float32
    ) * HD ** (-0.5)
    scores = jnp.where(allowed[:, None, None, :], scores, -jnp.inf)
    previous = highest.reshape(rows_here, heads_here, per_group)
    new_top = jnp.maximum(previous, jnp.max(scores, axis=-1))
    weights = jnp.exp(scores - new_top[..., None])
    factor = jnp.exp(previous - new_top)
    new_sum = weight_sum.reshape(rows_here, heads_here, per_group) * factor + jnp.sum(
        weights, axis=-1
    )
    partial_value = jnp.einsum(
        "tgjs,sgd->tgjd",
        weights.astype(jnp.bfloat16),
        value_heads,
        preferred_element_type=jnp.float32,
    )
    new_running = (
        running.reshape(rows_here, heads_here, per_group, width) * factor[..., None] + partial_value
    )
    return (
        new_running.reshape(rows_here, -1),
        new_top.reshape(rows_here, -1),
        new_sum.reshape(rows_here, -1),
    )


def block_allow(query_docs, block_docs, visits, anchor, holder, stride, rows_here, key_rows):
    blocks_q = rows_here // BLOCK
    blocks_k = key_rows // BLOCK
    query_doc = lax.dynamic_slice_in_dim(query_docs, anchor * blocks_q, blocks_q)
    block_doc = lax.dynamic_slice_in_dim(block_docs, holder * blocks_k, blocks_k)
    visited = lax.dynamic_slice_in_dim(visits, anchor * blocks_q, blocks_q)[:, stride, :]
    allowed = (visited == 1) & (query_doc[:, None] == block_doc[None, :])
    return jnp.repeat(jnp.repeat(allowed, BLOCK, axis=0), BLOCK, axis=1)


def shards(
    queries,
    context_keys,
    context_values,
    response_keys,
    response_values,
    out_weight,
    query_docs,
    block_docs,
    visits,
):
    rows_here = queries.shape[0]
    key_rows = context_keys.shape[0]
    heads_here = context_keys.shape[1] // HD
    per_group = HQ // KVH
    blk_count = lax.axis_size("blk")
    position = lax.axis_index("blk")
    query_heads = queries.reshape(rows_here, heads_here, per_group, HD)
    lanes = heads_here * per_group
    running = jnp.zeros((rows_here, lanes * HD), jnp.float32)
    highest = jnp.full((rows_here, lanes), -jnp.inf, jnp.float32)
    weight_sum = jnp.zeros((rows_here, lanes), jnp.float32)
    places = jnp.arange(rows_here)
    causal = places[:, None] >= places[None, :]
    running, highest, weight_sum = attend(
        running, highest, weight_sum, query_heads, response_keys, response_values, causal
    )
    key_block = context_keys
    value_block = context_values
    for stride in range(HOPS + 1):
        if stride > 0:
            key_block, value_block = from_behind((key_block, value_block), "blk", -1)
        holder = (position + stride) % blk_count
        allowed = block_allow(
            query_docs, block_docs, visits, position, holder, stride, rows_here, key_rows
        )
        running, highest, weight_sum = attend(
            running, highest, weight_sum, query_heads, key_block, value_block, allowed
        )
    attended = (
        (running.reshape(rows_here, lanes, HD) / weight_sum[:, :, None])
        .reshape(rows_here, -1)
        .astype(jnp.bfloat16)
    )
    products = jnp.dot(
        attended,
        lax.all_gather(out_weight, "blk", axis=1, tiled=True),
        preferred_element_type=jnp.float32,
    )
    mixed = lax.psum_scatter(products.astype(jnp.bfloat16), "head", scatter_dimension=1, tiled=True)
    return mixed


def solution(mesh):
    in_specs = (
        P("blk", "head"),
        P("blk", "head"),
        P("blk", "head"),
        P("blk", "head"),
        P("blk", "head"),
        P("head", "blk"),
        P(),
        P(),
        P(),
    )
    out_specs = P("blk", "head")
    return jax.shard_map(shards, mesh=mesh, in_specs=in_specs, out_specs=out_specs, check_vma=False)
```

profile of v0, /device:TPU:1, one launch (start us, length us, event | category | flops | bytes accessed | tf_op | source)
XLA Modules:
  0.0 247.4 jit_solution(1820500035767872004)
XLA Ops:
  6.5 0.7 all-gather.2.cloned.1.call-update
  7.3 1.5 collective-permute-start
  8.8 1.1 copy.19
  9.8 6.1 %collective-permute-start.1 = (bf16[1024,128]{0,1:T(8,128)(2,1)S(1)}, bf16[1024,128]{0,1:T(8,128)(2,1)S(1)}, u32[]{:S(2)}, u32[]{:S(2)}) collective-permute-start(bf16[1024,128]{0,1:T(8,128)(2,1)S(1)} %copy.19), channel_id=1, source_target_pairs={{0,120},{8,0},{16,8},{24,16},{32,24},{40,32},{48,40},{56,48},{64,5... | collective-permute-start | bytes 786440 | tf_op jit(solution)/shard_map/ppermute | solution.py:15
  16.0 0.8 dynamic-slice_compare_fusion.3
  16.8 0.1 copy.13
  16.9 0.1 copy.17
  17.1 0.1 copy.24
  17.2 0.7 dynamic_slice.25
  17.9 0.9 fusion.102
  19.0 1.3 fusion.103
  20.3 2.3 fusion.8
  22.6 0.3 fusion.28
  23.0 0.7 collective-permute-start.2
  23.7 0.7 collective-permute-start.3
  24.5 1.3 fusion.9
  25.9 10.3 %collective-permute-done.2 = bf16[1024,128]{1,0:T(8,128)(2,1)S(1)} collective-permute-done((bf16[1024,128]{1,0:T(8,128)(2,1)S(1)}, bf16[1024,128]{1,0:T(8,128)(2,1)S(1)}, u32[]{:S(2)}, u32[]{:S(2)}) %collective-permute-start.2) | collective-permute-done | bytes 262176 | tf_op jit(solution)/shard_map/ppermute | solution.py:15
  36.2 8.3 %collective-permute-done.3 = bf16[1024,128]{0,1:T(8,128)(2,1)S(1)} collective-permute-done((bf16[1024,128]{0,1:T(8,128)(2,1)S(1)}, bf16[1024,128]{0,1:T(8,128)(2,1)S(1)}, u32[]{:S(2)}, u32[]{:S(2)}) %collective-permute-start.3) | collective-permute-done | bytes 262176 | tf_op jit(solution)/shard_map/ppermute | solution.py:15
  44.6 4.6 %fusion.10 = (f32[256,8]{0,1:T(8,128)S(1)}, f32[1024,256,8]{1,0,2:T(8,128)}) fusion(pred[256,1024]{0,1:T(8,128)(4,1)S(1)} %bitcast.271, bf16[1024,128]{1,0:T(8,128)(2,1)S(1)} %collective-permute-done.2, bf16[256,1024]{1,0:T(8,128)(2,1)S(1)} %copy-done), kind=kOutput, calls=%fused_computation.19 | convolution fusion | flops 543160320 | bytes 9445376 | tf_op jit(solution)/shard_map/tgjd,sgd->tgjs/dot_general | solution.py:22
  49.3 1.3 fusion.11
  50.6 1.7 fusion
  52.3 1.7 fusion.2
  54.1 5.3 %fusion.4 = f32[256,8]{0,1:T(8,128)S(1)} fusion(f32[1024,256,8]{1,0,2:T(8,128)} %get-tuple-element.32, f32[256,8]{0,1:T(8,128)S(1)} %get-tuple-element.11, pred[256,1024]{0,1:T(8,128)(4,1)S(1)} %bitcast.272), kind=kLoop, calls=%fused_computation.13 | loop fusion | flops 8386560 | bytes 8667136 | tf_op jit(solution)/shard_map/reduce_sum | solution.py:30
  59.4 1.7 fusion.6
  61.2 0.5 fusion.64
  61.7 2.4 fusion.60
  64.1 2.3 fusion.57
  66.5 2.3 fusion.54
  68.8 2.3 fusion.51
  71.2 69.6 %all-gather.2.cloned.1.call-done = bf16[1024,8192]{1,0:T(8,128)(2,1)} async-done(((bf16[1024,512]{1,0:T(8,128)(2,1)}), bf16[1024,8192]{1,0:T(8,128)(2,1)}) %all-gather.2.cloned.1.call-update) | async-done | bytes 16777232 | tf_op jit(solution)/shard_map/all_gather | solution.py:105
  140.8 12.0 %convolution_convert_fusion = bf16[256,8192]{1,0:T(8,128)(2,1)} fusion(bf16[256,1024]{0,1:T(8,128)(2,1)S(1)} %fusion.67, bf16[1024,8192]{1,0:T(8,128)(2,1)} %all-gather.2.cloned.1.call-done), kind=kOutput, calls=%fused_computation | convolution fusion | flops 4297064448 | bytes 21495808 | tf_op jit(solution)/shard_map/dot_general | solution.py:103
  152.8 87.7 %reduce-scatter.2.cloned.1.call-done = bf16[256,1024]{1,0:T(8,128)(2,1)} async-done(((bf16[256,8192]{1,0:T(8,128)(2,1)}), bf16[256,1024]{1,0:T(8,128)(2,1)}) %reduce-scatter.2.cloned.1.call-update) | async-done | bytes 524304 | tf_op jit(solution)/shard_map/reduce_scatter | solution.py:108
  (34 shorter events, 0.9 us)
Async XLA Ops:
  6.5 12.4 %copy-start = (bf16[256,1024]{1,0:T(8,128)(2,1)S(1)}, bf16[256,1024]{1,0:T(8,128)(2,1)}, u32[]{:S(2)}) copy-start(bf16[256,1024]{1,0:T(8,128)(2,1)} %param.9) | copy-start | bytes 1572868
  6.5 134.2 %all-gather.2.cloned.1.call-start = ((), (), s32[]{:S(2)}) async-start(), calls=%async_computation.1 | async-start | bytes 17825792 | tf_op jit(solution)/shard_map/all_gather | solution.py:105
  7.3 233.3 %reduce-scatter.2.cloned.1.call-start = ((), (), s32[]{:S(2)}) async-start(), calls=%async_computation.2 | async-start | bytes 4718592 | tf_op jit(solution)/shard_map/reduce_scatter | solution.py:108
  7.3 15.7 %collective-permute-start = (bf16[1024,128]{1,0:T(8,128)(2,1)}, bf16[1024,128]{1,0:T(8,128)(2,1)S(1)}, u32[]{:S(2)}, u32[]{:S(2)}) collective-permute-start(bf16[1024,128]{1,0:T(8,128)(2,1)} %param.10), channel_id=1, source_target_pairs={{0,120},{8,0},{16,8},{24,16},{32,24},{40,32},{48,40},{56,48},{64,5... | collective-permute-start | bytes 786440 | tf_op jit(solution)/shard_map/ppermute | solution.py:15
  9.8 13.9 %collective-permute-start.1 = (bf16[1024,128]{0,1:T(8,128)(2,1)S(1)}, bf16[1024,128]{0,1:T(8,128)(2,1)S(1)}, u32[]{:S(2)}, u32[]{:S(2)}) collective-permute-start(bf16[1024,128]{0,1:T(8,128)(2,1)S(1)} %copy.19), channel_id=1, source_target_pairs={{0,120},{8,0},{16,8},{24,16},{32,24},{40,32},{48,40},{56,48},{64,5... | collective-permute-start | bytes 786440 | tf_op jit(solution)/shard_map/ppermute | solution.py:15
  23.0 13.2 %collective-permute-start.2 = (bf16[1024,128]{1,0:T(8,128)(2,1)S(1)}, bf16[1024,128]{1,0:T(8,128)(2,1)S(1)}, u32[]{:S(2)}, u32[]{:S(2)}) collective-permute-start(bf16[1024,128]{1,0:T(8,128)(2,1)S(1)} %collective-permute-done), channel_id=1, source_target_pairs={{0,120},{8,0},{16,8},{24,16},{32,24},{40,32},{48,40},{56,48},{64,5... | collective-permute-start | bytes 786440 | tf_op jit(solution)/shard_map/ppermute | solution.py:15
  23.7 20.8 %collective-permute-start.3 = (bf16[1024,128]{0,1:T(8,128)(2,1)S(1)}, bf16[1024,128]{0,1:T(8,128)(2,1)S(1)}, u32[]{:S(2)}, u32[]{:S(2)}) collective-permute-start(bf16[1024,128]{0,1:T(8,128)(2,1)S(1)} %collective-permute-done.1), channel_id=1, source_target_pairs={{0,120},{8,0},{16,8},{24,16},{32,24},{40,32},{48,40},{56,48},{64,5... | collective-permute-start | bytes 786440 | tf_op jit(solution)/shard_map/ppermute | solution.py:15
  36.2 13.0 %collective-permute-start.4 = (bf16[1024,128]{1,0:T(8,128)(2,1)S(1)}, bf16[1024,128]{1,0:T(8,128)(2,1)S(1)}, u32[]{:S(2)}, u32[]{:S(2)}) collective-permute-start(bf16[1024,128]{1,0:T(8,128)(2,1)S(1)} %collective-permute-done.2), channel_id=1, source_target_pairs={{0,120},{8,0},{16,8},{24,16},{32,24},{40,32},{48,40},{56,48},{64,5... | collective-permute-start | bytes 786440 | tf_op jit(solution)/shard_map/ppermute | solution.py:15
  44.5 24.3 %collective-permute-start.5 = (bf16[1024,128]{0,1:T(8,128)(2,1)S(1)}, bf16[1024,128]{0,1:T(8,128)(2,1)S(1)}, u32[]{:S(2)}, u32[]{:S(2)}) collective-permute-start(bf16[1024,128]{0,1:T(8,128)(2,1)S(1)} %collective-permute-done.3), channel_id=1, source_target_pairs={{0,120},{8,0},{16,8},{24,16},{32,24},{40,32},{48,40},{56,48},{64,5... | collective-permute-start | bytes 786440 | tf_op jit(solution)/shard_map/ppermute | solution.py:15
  54.0 7.1 %copy-start.3 = (bf16[256,128]{1,0:T(8,128)(2,1)S(1)}, bf16[256,128]{1,0:T(8,128)(2,1)}, u32[]{:S(2)}) copy-start(bf16[256,128]{1,0:T(8,128)(2,1)} %param.13) | copy-start | bytes 196612
  54.1 7.6 %copy-start.2 = (bf16[1024,128]{1,0:T(8,128)(2,1)S(1)}, bf16[1024,128]{1,0:T(8,128)(2,1)}, u32[]{:S(2)}) copy-start(bf16[1024,128]{1,0:T(8,128)(2,1)} %param.11) | copy-start | bytes 786436
  61.2 5.3 %slice-start = ((s8[8388608]{0:T(1024)(128)(4,1)}), s8[4194304]{0:T(1024)(128)(4,1)S(1)}, s32[]{:S(2)}) async-start(s8[8388608]{0:T(1024)(128)(4,1)} %bitcast.260), calls=%async_computation.3 | async-start | bytes 8388608
  61.7 4.8 %slice-start.1 = ((s8[8388608]{0:T(1024)(128)(4,1)}), s8[4194304]{0:T(1024)(128)(4,1)S(1)}, s32[]{:S(2)}) async-start(s8[8388608]{0:T(1024)(128)(4,1)} %bitcast.260), calls=%async_computation.4 | async-start | bytes 8388608
  71.1 169.5 %copy-start.1 = (bf16[256,1024]{1,0:T(8,128)(2,1)S(1)}, bf16[256,1024]{1,0:T(8,128)(2,1)}, u32[]{:S(2)}) copy-start(bf16[256,1024]{1,0:T(8,128)(2,1)} %param.9) | copy-start | bytes 1572868
Sparse Core Ops, SparseCore 0:
  9.7 131.0 all-gather.1
  153.0 87.5 reduce-scatter.1
where the time goes:
time: 248 us; the launch traced here: 247 us
  waiting for transfers between devices  177 us (71%)
  matrix products  32.7 us (13%)
  between operations  13.7 us (6%)
  other arithmetic  11.8 us (5%)
  starting transfers between devices  9.01 us (4%)
  local copies, waits for them, and re-layouts  3.55 us (1%)
    reduce_scatter x1, waiting for transfers between devices, shards(): lax.psum_scatter(products.astype(jnp.bfloat16), 'head', scatter_dimension...  87.7 us
    all_gather x1, waiting for transfers between devices, shards(): lax.all_gather(out_weight, 'blk', axis=1, tiled=True)  69.6 us
    ppermute x6, waiting for transfers between devices, from_behind(): lax.ppermute(value, axis, [(i, (i + by) % devices) for i in range(devices)])  18.7 us
    dot_general x1, matrix products, shards(): jnp.dot(attended, lax.all_gather(out_weight, 'blk', axis=1, tiled=True),...  12 us
    dot_general x5, matrix products, attend(): jnp.einsum('tgjd,sgd->tgjs', query_heads, key_heads, preferred_element_ty...  10.8 us
    reduce_sum x5, other arithmetic, attend(): jnp.sum(weights, axis=-1)  10.7 us
    dot_general x5, matrix products, attend(): jnp.einsum('tgjs,sgd->tgjd', weights.astype(jnp.bfloat16), value_heads, p...  9.86 us
    ppermute x6, starting transfers between devices, from_behind(): lax.ppermute(value, axis, [(i, (i + by) % devices) for i in range(devices)])  8.97 us
  transfers between devices with their start and end apart: 8, of which 4 were waited for; matrix products, arithmetic and copies ran while one was open for 15% of the time, Pallas kernels for 0%

commit v1 on v0

--- a/solution.py
+++ b/solution.py
@@ -100,11 +100,11 @@
         .reshape(rows_here, -1)
         .astype(jnp.bfloat16)
     )
-    products = jnp.dot(
-        attended,
-        lax.all_gather(out_weight, "blk", axis=1, tiled=True),
-        preferred_element_type=jnp.float32,
+    store_things = lambda message, pos_dim: jnp.concatenate(
+        lax.all_to_all(jnp.stack([message for _ in range(lax.axis_size("blk"))]), "blk", 0, 0),
+        axis=pos_dim,
     )
+    products = jnp.dot(attended, store_things(out_weight, 1), preferred_element_type=jnp.float32)
     mixed = lax.psum_scatter(products.astype(jnp.bfloat16), "head", scatter_dimension=1, tiled=True)
     return mixed
 

time: 248 us -> 358 us (1.44)
  waiting for transfers between devices: 177 us -> 279 us
  starting transfers between devices: 9.01 us -> 17.3 us
  local copies, waits for them, and re-layouts: 3.55 us -> 8.7 us
  matrix products: 32.7 us -> 28.6 us
    ppermute x6, waiting for transfers between devices: 18.7 us -> 187 us  [from_behind(): lax.ppermute(value, axis, [(i, (i + by) % devices) for i in range(devices)])]
    all_gather x1 -> x0, waiting for transfers between devices: 69.6 us -> none  [shards(): lax.all_gather(out_weight, 'blk', axis=1, tiled=True)]
    all_to_all x0 -> x1, starting transfers between devices: none -> 9.42 us  [shards(): lax.all_to_all(jnp.stack([message for _ in range(lax.axis_size('blk'))]),...]
    another operation x0 -> x1, local copies, waits for them, and re-layouts: none -> 5.98 us  [shards(): jnp.stack([message for _ in range(lax.axis_size('blk'))])]
  transfers between devices with their start and end apart: 8 -> 8, of which waited for: 4 -> 5; matrix products, arithmetic and copies ran while one was open for 15% -> 9% of each run, Pallas kernels for 0% -> 0%
where the time goes in v1:
time: 358 us
  waiting for transfers between devices  279 us (78%)
  matrix products  28.6 us (8%)
  starting transfers between devices  17.3 us (5%)
  between operations  13.7 us (4%)
  other arithmetic  10.8 us (3%)
  local copies, waits for them, and re-layouts  8.7 us (2%)
    ppermute x6, waiting for transfers between devices, from_behind(): lax.ppermute(value, axis, [(i, (i + by) % devices) for i in range(devices)])  187 us
    reduce_scatter x1, waiting for transfers between devices, shards(): lax.psum_scatter(products.astype(jnp.bfloat16), 'head', scatter_dimension...  91.1 us
    reduce_sum x5, other arithmetic, attend(): jnp.sum(weights, axis=-1)  10.6 us
    dot_general x5, matrix products, attend(): jnp.einsum('tgjs,sgd->tgjd', weights.astype(jnp.bfloat16), value_heads, p...  9.88 us
    dot_general x1, matrix products, shards(): jnp.dot(attended, store_things(out_weight, 1), preferred_element_type=jnp...  9.64 us
    all_to_all x1, starting transfers between devices, shards(): lax.all_to_all(jnp.stack([message for _ in range(lax.axis_size('blk'))]),...  9.42 us
    dot_general x5, matrix products, attend(): jnp.einsum('tgjd,sgd->tgjs', query_heads, key_heads, preferred_element_ty...  9.06 us
    ppermute x6, starting transfers between devices, from_behind(): lax.ppermute(value, axis, [(i, (i + by) % devices) for i in range(devices)])  7.81 us
  transfers between devices with their start and end apart: 8, of which 5 were waited for; matrix products, arithmetic and copies ran while one was open for 9% of the time, Pallas kernels for 0%

profile of v1, /device:TPU:1, one launch (start us, length us, event | category | flops | bytes accessed | tf_op | source)
XLA Modules:
  0.0 357.6 jit_solution(16802652298314236321)
XLA Ops:
  6.5 1.5 copy.44
  8.1 6.0 %stack.2 = bf16[16,1024,512]{1,2,0:T(8,128)(2,1)} broadcast(bf16[1024,512]{0,1:T(8,128)(2,1)S(1)} %copy.44), dimensions={1,2} | broadcast | bytes 17825792 | tf_op jit(solution)/shard_map/stack | solution.py:104
  14.1 9.4 %all-to-all-start = ((bf16[16,1024,512]{1,2,0:T(8,128)(2,1)}), bf16[16,1024,512]{1,2,0:T(8,128)(2,1)}, u32[]{:S(2)}, u32[]{:S(2)}) async-start(bf16[16,1024,512]{1,2,0:T(8,128)(2,1)} %stack.2), calls=%async_computation | async-start | bytes 33554432 | tf_op jit(solution)/shard_map/all_to_all | solution.py:104
  23.6 0.2 collective-permute-start
  23.8 0.1 copy.36
  24.0 5.3 %collective-permute-start.1 = (bf16[1024,128]{0,1:T(8,128)(2,1)S(1)}, bf16[1024,128]{0,1:T(8,128)(2,1)S(1)}, u32[]{:S(2)}, u32[]{:S(2)}) collective-permute-start(bf16[1024,128]{0,1:T(8,128)(2,1)S(1)} %copy.36), channel_id=1, source_target_pairs={{0,120},{8,0},{16,8},{24,16},{32,24},{40,32},{48,40},{56,48},{64,5... | collective-permute-start | bytes 786440 | tf_op jit(solution)/shard_map/ppermute | solution.py:15
  29.3 0.1 copy.30
  29.4 0.1 copy.34
  29.5 0.1 copy.38
  29.6 0.1 copy.41
  30.1 0.5 fusion.104
  30.6 1.3 fusion.8
  32.0 0.3 fusion.28
  32.3 178.9 %collective-permute-done = bf16[1024,128]{1,0:T(8,128)(2,1)S(1)} collective-permute-done((bf16[1024,128]{1,0:T(8,128)(2,1)S(1)}, bf16[1024,128]{1,0:T(8,128)(2,1)S(1)}, u32[]{:S(2)}, u32[]{:S(2)}) %collective-permute-start) | collective-permute-done | bytes 262176 | tf_op jit(solution)/shard_map/ppermute | solution.py:15
  211.2 2.8 collective-permute-done.1
  214.2 1.3 fusion.9
  215.5 3.0 collective-permute-done.2
  218.5 2.8 collective-permute-done.3
  221.3 2.2 collective-permute-start.5
  223.6 4.6 %fusion.10 = (f32[256,8]{0,1:T(8,128)S(1)}, f32[1024,256,8]{1,0,2:T(8,128)}) fusion(pred[256,1024]{0,1:T(8,128)(4,1)S(1)} %bitcast.275, bf16[1024,128]{1,0:T(8,128)(2,1)S(1)} %collective-permute-done.2, bf16[256,1024]{1,0:T(8,128)(2,1)S(1)} %copy-done), kind=kOutput, calls=%fused_computation.19 | convolution fusion | flops 543160320 | bytes 9445376 | tf_op jit(solution)/shard_map/tgjd,sgd->tgjs/dot_general | solution.py:22
  228.2 1.3 fusion.11
  229.6 1.7 fusion
  231.3 1.7 fusion.2
  233.0 5.2 %fusion.4 = f32[256,8]{0,1:T(8,128)S(1)} fusion(f32[1024,256,8]{1,0,2:T(8,128)} %get-tuple-element.32, f32[256,8]{0,1:T(8,128)S(1)} %get-tuple-element.11, pred[256,1024]{0,1:T(8,128)(4,1)S(1)} %bitcast.276), kind=kLoop, calls=%fused_computation.13 | loop fusion | flops 8386560 | bytes 8667136 | tf_op jit(solution)/shard_map/reduce_sum | solution.py:30
  238.2 1.7 fusion.6
  240.0 0.5 fusion.64
  240.5 2.4 fusion.60
  242.9 2.3 fusion.57
  245.3 2.3 fusion.54
  247.6 2.3 divide_convert_fusion
  250.0 9.6 %convolution_convert_fusion = bf16[256,8192]{1,0:T(8,128)(2,1)} fusion(bf16[256,1024]{0,1:T(8,128)(2,1)S(1)} %bitcast.278, bf16[1024,8192]{0,1:T(8,128)(2,1)} %bitcast.50), kind=kOutput, calls=%fused_computation | convolution fusion | flops 4297064448 | bytes 21495808 | tf_op jit(solution)/shard_map/dot_general | solution.py:107
  259.6 91.1 %reduce-scatter.2.cloned.1.call-done = bf16[256,1024]{1,0:T(8,128)(2,1)} async-done(((bf16[256,8192]{1,0:T(8,128)(2,1)}), bf16[256,1024]{1,0:T(8,128)(2,1)}) %reduce-scatter.2.cloned.1.call-update) | async-done | bytes 524304 | tf_op jit(solution)/shard_map/reduce_scatter | solution.py:108
  (44 shorter events, 1.0 us)
Async XLA Ops:
  6.5 23.5 %copy-start = (bf16[256,1024]{1,0:T(8,128)(2,1)S(1)}, bf16[256,1024]{1,0:T(8,128)(2,1)}, u32[]{:S(2)}) copy-start(bf16[256,1024]{1,0:T(8,128)(2,1)} %param.9) | copy-start | bytes 1572868
  14.1 9.5 %copy-start.2 = (bf16[1024,128]{1,0:T(8,128)(2,1)S(1)}, bf16[1024,128]{1,0:T(8,128)(2,1)}, u32[]{:S(2)}) copy-start(bf16[1024,128]{1,0:T(8,128)(2,1)} %param.10) | copy-start | bytes 786436
  14.1 9.7 %copy-start.3 = (bf16[1024,128]{1,0:T(8,128)(2,1)S(1)}, bf16[1024,128]{1,0:T(8,128)(2,1)}, u32[]{:S(2)}) copy-start(bf16[1024,128]{1,0:T(8,128)(2,1)} %param.11) | copy-start | bytes 786436
  14.1 15.2 %copy-start.6 = (s32[32,4,8]{0,2,1:T(8,128)S(1)}, s32[32,4,8]{0,2,1:T(8,128)}, u32[]{:S(2)}) copy-start(s32[32,4,8]{0,2,1:T(8,128)} %param.17) | copy-start | bytes 12292
  14.1 15.6 %copy-start.8 = (s32[32]{0:T(128)S(1)}, s32[32]{0:T(128)}, u32[]{:S(2)}) copy-start(s32[32]{0:T(128)} %param.15) | copy-start | bytes 388
  14.1 15.7 %copy-start.7 = (s32[128]{0:T(128)S(1)}, s32[128]{0:T(128)}, u32[]{:S(2)}) copy-start(s32[128]{0:T(128)} %param.16) | copy-start | bytes 1540
  14.1 16.0 %copy-start.4 = (bf16[256,128]{1,0:T(8,128)(2,1)S(1)}, bf16[256,128]{1,0:T(8,128)(2,1)}, u32[]{:S(2)}) copy-start(bf16[256,128]{1,0:T(8,128)(2,1)} %param.12) | copy-start | bytes 196612
  14.1 235.8 %all-to-all-start = ((bf16[16,1024,512]{1,2,0:T(8,128)(2,1)}), bf16[16,1024,512]{1,2,0:T(8,128)(2,1)}, u32[]{:S(2)}, u32[]{:S(2)}) async-start(bf16[16,1024,512]{1,2,0:T(8,128)(2,1)} %stack.2), calls=%async_computation | async-start | bytes 33554432 | tf_op jit(solution)/shard_map/all_to_all | solution.py:104
  23.5 327.2 %reduce-scatter.2.cloned.1.call-start = ((), (), s32[]{:S(2)}) async-start(), calls=%async_computation.2 | async-start | bytes 4718592 | tf_op jit(solution)/shard_map/reduce_scatter | solution.py:108
  23.6 187.6 %collective-permute-start = (bf16[1024,128]{1,0:T(8,128)(2,1)S(1)}, bf16[1024,128]{1,0:T(8,128)(2,1)S(1)}, u32[]{:S(2)}, u32[]{:S(2)}) collective-permute-start(bf16[1024,128]{1,0:T(8,128)(2,1)S(1)} %copy-done.2), channel_id=1, source_target_pairs={{0,120},{8,0},{16,8},{24,16},{32,24},{40,32},{48,40},{56,48},{64,5... | collective-permute-start | bytes 786440 | tf_op jit(solution)/shard_map/ppermute | solution.py:15
  24.0 190.1 %collective-permute-start.1 = (bf16[1024,128]{0,1:T(8,128)(2,1)S(1)}, bf16[1024,128]{0,1:T(8,128)(2,1)S(1)}, u32[]{:S(2)}, u32[]{:S(2)}) collective-permute-start(bf16[1024,128]{0,1:T(8,128)(2,1)S(1)} %copy.36), channel_id=1, source_target_pairs={{0,120},{8,0},{16,8},{24,16},{32,24},{40,32},{48,40},{56,48},{64,5... | collective-permute-start | bytes 786440 | tf_op jit(solution)/shard_map/ppermute | solution.py:15
  211.2 7.3 %collective-permute-start.2 = (bf16[1024,128]{1,0:T(8,128)(2,1)S(1)}, bf16[1024,128]{1,0:T(8,128)(2,1)S(1)}, u32[]{:S(2)}, u32[]{:S(2)}) collective-permute-start(bf16[1024,128]{1,0:T(8,128)(2,1)S(1)} %collective-permute-done), channel_id=1, source_target_pairs={{0,120},{8,0},{16,8},{24,16},{32,24},{40,32},{48,40},{56,48},{64,5... | collective-permute-start | bytes 786440 | tf_op jit(solution)/shard_map/ppermute | solution.py:15
  214.0 7.3 %collective-permute-start.3 = (bf16[1024,128]{0,1:T(8,128)(2,1)S(1)}, bf16[1024,128]{0,1:T(8,128)(2,1)S(1)}, u32[]{:S(2)}, u32[]{:S(2)}) collective-permute-start(bf16[1024,128]{0,1:T(8,128)(2,1)S(1)} %collective-permute-done.1), channel_id=1, source_target_pairs={{0,120},{8,0},{16,8},{24,16},{32,24},{40,32},{48,40},{56,48},{64,5... | collective-permute-start | bytes 786440 | tf_op jit(solution)/shard_map/ppermute | solution.py:15
  218.5 9.6 %collective-permute-start.4 = (bf16[1024,128]{1,0:T(8,128)(2,1)S(1)}, bf16[1024,128]{1,0:T(8,128)(2,1)S(1)}, u32[]{:S(2)}, u32[]{:S(2)}) collective-permute-start(bf16[1024,128]{1,0:T(8,128)(2,1)S(1)} %collective-permute-done.2), channel_id=1, source_target_pairs={{0,120},{8,0},{16,8},{24,16},{32,24},{40,32},{48,40},{56,48},{64,5... | collective-permute-start | bytes 786440 | tf_op jit(solution)/shard_map/ppermute | solution.py:15
  221.3 26.3 %collective-permute-start.5 = (bf16[1024,128]{0,1:T(8,128)(2,1)S(1)}, bf16[1024,128]{0,1:T(8,128)(2,1)S(1)}, u32[]{:S(2)}, u32[]{:S(2)}) collective-permute-start(bf16[1024,128]{0,1:T(8,128)(2,1)S(1)} %collective-permute-done.3), channel_id=1, source_target_pairs={{0,120},{8,0},{16,8},{24,16},{32,24},{40,32},{48,40},{56,48},{64,5... | collective-permute-start | bytes 786440 | tf_op jit(solution)/shard_map/ppermute | solution.py:15
  233.0 6.9 %copy-start.5 = (bf16[256,128]{1,0:T(8,128)(2,1)S(1)}, bf16[256,128]{1,0:T(8,128)(2,1)}, u32[]{:S(2)}) copy-start(bf16[256,128]{1,0:T(8,128)(2,1)} %param.13) | copy-start | bytes 196612
  240.0 5.3 %slice-start = ((s8[8388608]{0:T(1024)(128)(4,1)}), s8[4194304]{0:T(1024)(128)(4,1)S(1)}, s32[]{:S(2)}) async-start(s8[8388608]{0:T(1024)(128)(4,1)} %bitcast.264), calls=%async_computation.3 | async-start | bytes 8388608
  240.5 4.8 %slice-start.1 = ((s8[8388608]{0:T(1024)(128)(4,1)}), s8[4194304]{0:T(1024)(128)(4,1)S(1)}, s32[]{:S(2)}) async-start(s8[8388608]{0:T(1024)(128)(4,1)} %bitcast.264), calls=%async_computation.4 | async-start | bytes 8388608
  249.9 100.8 %copy-start.1 = (bf16[256,1024]{1,0:T(8,128)(2,1)S(1)}, bf16[256,1024]{1,0:T(8,128)(2,1)}, u32[]{:S(2)}) copy-start(bf16[256,1024]{1,0:T(8,128)(2,1)} %param.9) | copy-start | bytes 1572868
Sparse Core Ops, SparseCore 0:
  259.7 90.9 reduce-scatter.1
